TPU v7x, 256 devices: a whole 4x4x8 slice. The times are simulated.
256 devices in a mesh: days: 128 (over x, z, y), cols: 2 (over core).
Axes of the slice: x: 4, y: 4, z: 8, core: 2. Of those that a mesh axis runs over, the one named last changes fastest.
Arguments:
- cube: float32 [4096, 65536], P('days', 'cols'), may hold values from -800 to 800
- year_id: int32 [4096], P('days'), may hold values from 0 to 2, as said below
- parent: int32 [65536], P('cols'), may hold values from 0 to 511
Outputs:
- running: float32 [4096, 65536], P('days', 'cols')
- rollup: float32 [4096, 512], P('days', 'cols')
Inputs may be any that keep to these rules, and one draw needn't show every extreme that they name: year_id never falls from one day to the next; every year of 0 to 2 has 1 to 3072 days.
All inputs are finite; a program needn't handle non-finite values.
Results may differ from a plain program's by a relative error of at most 0.00012.
Values sent between devices are 32-bit elements; how exact they have to be, the bound alone decides.
A program may use at most 128 MiB of HBM per device.

v0:
```python
import math

import jax
import jax.numpy as jnp
from jax import lax
from jax.sharding import Mesh
from jax.sharding import PartitionSpec as P

PARENTS = 512
DAYS = ("days_0", "days_1", "days_2")


def side_by_side(arrays, axis, dim, along):
    widths = [math.prod(a.shape[along:]) for a in arrays]
    both = jnp.concatenate(
        [a.reshape(*a.shape[:along], w) for a, w in zip(arrays, widths)], axis=along
    )
    out = lax.all_gather(both, axis, axis=dim, tiled=True)
    tiles = jnp.split(out, [sum(widths[:k]) for k in range(1, len(widths))], axis=along)
    return tuple((b.reshape(*out.shape[:along], *a.shape[along:]) for a, b in zip(arrays, tiles)))


def from_everyone(array, axis):
    peers = lax.axis_size(axis)
    return lax.all_to_all(
        jnp.broadcast_to(array[None], (peers, *array.shape)), axis, 0, 0, tiled=True
    )


def over_copies(array, axis):
    everything = from_everyone(array, axis)
    return jnp.sum(everything, axis=0)


def one_axis_at_a_time(array, axes):
    for axis in axes:
        array = lax.psum(array, axis)
    return array


def parent_totals(ytd, parent):
    width = ytd.shape[1]
    block = min(width, 4096)
    nblocks = width // block
    targets = jnp.arange(PARENTS, dtype=jnp.int32)

    def add_block(index, total):
        begin = (index * block).astype(jnp.int32)
        rows = lax.dynamic_slice_in_dim(ytd, begin, block, 1)
        owners = lax.dynamic_slice_in_dim(parent, begin, block, 0)
        onehot = (owners[:, None] == targets[None, :]).astype(jnp.float32)
        return total + jnp.dot(
            rows, onehot, preferred_element_type=jnp.float32, precision=lax.Precision.HIGHEST
        )

    start = jnp.zeros((ytd.shape[0], PARENTS), jnp.float32)
    return lax.fori_loop(0, nblocks, add_block, start)


def body(cube, year_id, parent):
    day_count = cube.shape[0]
    years = year_id.astype(jnp.float32)
    order = jnp.arange(day_count, dtype=jnp.int32)
    lower = jnp.logical_and(order[None, :] <= order[:, None], years[None, :] == years[:, None])
    local = jnp.dot(
        lower.astype(jnp.float32),
        cube,
        preferred_element_type=jnp.float32,
        precision=lax.Precision.HIGHEST,
    )
    first = years[:1]
    last = years[-1:]
    tail = local[-1]
    mine = lax.axis_index(DAYS)
    lasts, tails = side_by_side((last, tail[None, :]), DAYS, 0, 1)
    index = jnp.arange(lasts.shape[0], dtype=jnp.int32)
    weights = jnp.logical_and(index < mine, lasts == first[0]).astype(jnp.float32)
    carried = jnp.dot(
        weights[None, :], tails, preferred_element_type=jnp.float32, precision=lax.Precision.HIGHEST
    )[0]
    ytd = local + jnp.where(years[:, None] == first[0], carried[None, :], 0.0)
    partial_region = parent_totals(ytd, parent)
    total_days = day_count * lax.axis_size(DAYS)
    whole = over_copies(partial_region, "cols")
    squares = one_axis_at_a_time(jnp.sum(whole * whole), DAYS)
    share = PARENTS // lax.axis_size("cols")
    region = lax.dynamic_slice_in_dim(whole, lax.axis_index("cols") * share, share, 1)
    scale = jnp.sqrt(squares / (total_days * PARENTS) + 1e-06)
    return (ytd / scale, region / scale)


def solution(mesh):
    finer = Mesh(
        mesh.devices.reshape(4, 8, 4, mesh.shape["cols"]), ("days_0", "days_1", "days_2", "cols")
    )
    return jax.shard_map(
        body,
        mesh=finer,
        in_specs=(P(DAYS, "cols"), P(DAYS), P("cols")),
        out_specs=(P(DAYS, "cols"), P(DAYS, "cols")),
        check_vma=False,
    )
```

profile of v0, /device:TPU:2, one launch (start us, length us, event | category | flops | bytes accessed | tf_op | source)
XLA Modules:
  0.0 313.8 jit_solution(10033284970401329339)
XLA Ops:
  7.2 0.7 convert_element_type.8
  8.5 4.5 %fusion.10 = f32[32,32768]{1,0:T(8,128)S(1)} fusion(f32[32,32768]{1,0:T(8,128)} %param.5, f32[32]{0:T(128)S(1)} %convert_element_type.8), kind=kOutput, calls=%fused_computation.16 | convolution fusion | flops 402656256 | bytes 8388736 | tf_op jit(solution)/shard_map/dot_general | solution.py:65
  12.9 2.0 copy-done
  15.1 1.6 maximum_bitcast_fusion
  16.8 0.6 broadcast_compare_fusion
  17.4 152.5 %all-gather.3.cloned.1.call-done = f32[128,1,32769]{2,1,0:T(1,128)} async-done(((f32[1,1,32769]{2,1,0:T(1,128)}), f32[128,1,32769]{2,1,0:T(1,128)}) %all-gather.3.cloned.1.call-update) | async-done | bytes 16777744 | tf_op jit(solution)/shard_map/all_gather | solution.py:18
  169.9 34.6 %copy.7 = f32[128,1,32769]{0,2,1:T(8,128)} copy(f32[128,1,32769]{2,1,0:T(1,128)} %all-gather.3.cloned.1.call-done) | data formatting | bytes 33555456 | tf_op jit(solution)/shard_map/all_gather | solution.py:18
  204.5 14.8 %fusion.7 = f32[1,32768]{1,0:T(1,128)S(1)} fusion(f32[128,32769]{0,1:T(8,128)} %bitcast.15, f32[]{:T(128)} %bitcast, s32[]{:T(128)S(6)} %add.53), kind=kOutput, calls=%fused_computation.7 | convolution fusion | flops 50332032 | bytes 16909316 | tf_op jit(solution)/shard_map/dot_general | solution.py:78
  219.3 2.4 select_add_fusion
  221.7 38.6 %while.14 = (s32[]{:T(128)}, f32[32,512]{1,0:T(8,128)S(1)}, f32[32,32768]{1,0:T(8,128)}, s32[32768]{0:T(1024)}, s32[]{:T(128)}, /*index=5*/s32[]{:T(128)}, s32[]{:T(128)}, s32[]{:T(128)}) while((s32[]{:T(128)}, f32[32,512]{1,0:T(8,128)S(1)}, f32[32,32768]{1,0:T(8,128)}, s32[32768]{0:T(1024)}, s32[]{:T(128)}, /*index=5*/s32[]{:T(128)}, ...), condition=%wide.region_1.2_spmd.clone, body=%wide.region_0.1_spmd.clone.sunk | while | flops 807436288 | bytes 704661 | solution.py:57
  221.7 0.7 dynamic_slice.26
  222.4 4.1 %fusion.27 = f32[32,512]{1,0:T(8,128)S(1)} fusion(s32[4096]{0:T(1024)S(1)} %dynamic_slice.26, f32[32,32768]{1,0:T(8,128)} %get-tuple-element.167, s32[]{:T(128)S(6)} %select_n.22, f32[32,512]{1,0:T(8,128)S(1)} %get-tuple-element.158, pred[]{:T(512)S(6)} %compare.3), kind=kOutput, calls=%fused_computation.4.clone.1 | convolution fusion | flops 807436288 | bytes 671749 | tf_op jit(solution)/shard_map/while/body/eval_jaxpr/dot_general | solution.py:52
  226.5 0.7 dynamic_slice.26
  227.3 4.1 %fusion.27 = f32[32,512]{1,0:T(8,128)S(1)} fusion(s32[4096]{0:T(1024)S(1)} %dynamic_slice.26, f32[32,32768]{1,0:T(8,128)} %get-tuple-element.167, s32[]{:T(128)S(6)} %select_n.22, f32[32,512]{1,0:T(8,128)S(1)} %get-tuple-element.158, pred[]{:T(512)S(6)} %compare.3), kind=kOutput, calls=%fused_computation.4.clone.1 | convolution fusion | flops 807436288 | bytes 671749 | tf_op jit(solution)/shard_map/while/body/eval_jaxpr/dot_general | solution.py:52
  231.4 0.7 dynamic_slice.26
  232.1 4.1 %fusion.27 = f32[32,512]{1,0:T(8,128)S(1)} fusion(s32[4096]{0:T(1024)S(1)} %dynamic_slice.26, f32[32,32768]{1,0:T(8,128)} %get-tuple-element.167, s32[]{:T(128)S(6)} %select_n.22, f32[32,512]{1,0:T(8,128)S(1)} %get-tuple-element.158, pred[]{:T(512)S(6)} %compare.3), kind=kOutput, calls=%fused_computation.4.clone.1 | convolution fusion | flops 807436288 | bytes 671749 | tf_op jit(solution)/shard_map/while/body/eval_jaxpr/dot_general | solution.py:52
  236.2 0.7 dynamic_slice.26
  236.9 4.1 %fusion.27 = f32[32,512]{1,0:T(8,128)S(1)} fusion(s32[4096]{0:T(1024)S(1)} %dynamic_slice.26, f32[32,32768]{1,0:T(8,128)} %get-tuple-element.167, s32[]{:T(128)S(6)} %select_n.22, f32[32,512]{1,0:T(8,128)S(1)} %get-tuple-element.158, pred[]{:T(512)S(6)} %compare.3), kind=kOutput, calls=%fused_computation.4.clone.1 | convolution fusion | flops 807436288 | bytes 671749 | tf_op jit(solution)/shard_map/while/body/eval_jaxpr/dot_general | solution.py:52
  241.0 0.7 dynamic_slice.26
  241.8 4.1 %fusion.27 = f32[32,512]{1,0:T(8,128)S(1)} fusion(s32[4096]{0:T(1024)S(1)} %dynamic_slice.26, f32[32,32768]{1,0:T(8,128)} %get-tuple-element.167, s32[]{:T(128)S(6)} %select_n.22, f32[32,512]{1,0:T(8,128)S(1)} %get-tuple-element.158, pred[]{:T(512)S(6)} %compare.3), kind=kOutput, calls=%fused_computation.4.clone.1 | convolution fusion | flops 807436288 | bytes 671749 | tf_op jit(solution)/shard_map/while/body/eval_jaxpr/dot_general | solution.py:52
  245.9 0.7 dynamic_slice.26
  246.6 4.1 %fusion.27 = f32[32,512]{1,0:T(8,128)S(1)} fusion(s32[4096]{0:T(1024)S(1)} %dynamic_slice.26, f32[32,32768]{1,0:T(8,128)} %get-tuple-element.167, s32[]{:T(128)S(6)} %select_n.22, f32[32,512]{1,0:T(8,128)S(1)} %get-tuple-element.158, pred[]{:T(512)S(6)} %compare.3), kind=kOutput, calls=%fused_computation.4.clone.1 | convolution fusion | flops 807436288 | bytes 671749 | tf_op jit(solution)/shard_map/while/body/eval_jaxpr/dot_general | solution.py:52
  250.7 0.7 dynamic_slice.26
  251.4 4.1 %fusion.27 = f32[32,512]{1,0:T(8,128)S(1)} fusion(s32[4096]{0:T(1024)S(1)} %dynamic_slice.26, f32[32,32768]{1,0:T(8,128)} %get-tuple-element.167, s32[]{:T(128)S(6)} %select_n.22, f32[32,512]{1,0:T(8,128)S(1)} %get-tuple-element.158, pred[]{:T(512)S(6)} %compare.3), kind=kOutput, calls=%fused_computation.4.clone.1 | convolution fusion | flops 807436288 | bytes 671749 | tf_op jit(solution)/shard_map/while/body/eval_jaxpr/dot_general | solution.py:52
  255.5 0.7 dynamic_slice.26
  256.3 4.1 %fusion.27 = f32[32,512]{1,0:T(8,128)S(1)} fusion(s32[4096]{0:T(1024)S(1)} %dynamic_slice.26, f32[32,32768]{1,0:T(8,128)} %get-tuple-element.167, s32[]{:T(128)S(6)} %select_n.22, f32[32,512]{1,0:T(8,128)S(1)} %get-tuple-element.158, pred[]{:T(512)S(6)} %compare.3), kind=kOutput, calls=%fused_computation.4.clone.1 | convolution fusion | flops 807436288 | bytes 671749 | tf_op jit(solution)/shard_map/while/body/eval_jaxpr/dot_general | solution.py:52
  260.4 3.8 %all_to_all.5 = f32[2,32,512]{2,1,0:T(8,128)S(1)} all-to-all(f32[2,32,512]{2,1,0:T(8,128)S(1)} %broadcast_in_dim.45), channel_id=1, replica_groups=mesh['days_0'=4,'days_1'=8,'days_2'=4,'cols'=2] {'cols'}, dimensions={0} | all-to-all | bytes 262144 | tf_op jit(solution)/shard_map/all_to_all | solution.py:25
  264.8 9.2 %psum.21 = f32[]{:T(128)} all-reduce(f32[]{:T(128)} %multiply_reduce_fusion), channel_id=1, replica_groups=mesh['days_0'=4,'days_1'=8,'days_2'=4,'cols'=2] {'days_0'}, use_global_device_ids=true, to_apply=%region_4.5 | all-reduce | flops 1 | bytes 8 | tf_op jit(solution)/shard_map/psum | solution.py:37
  274.0 16.1 %psum.22 = f32[]{:T(128)} all-reduce(f32[]{:T(128)} %psum.21), channel_id=1, replica_groups=mesh['days_0'=4,'days_1'=8,'days_2'=4,'cols'=2] {'days_1'}, use_global_device_ids=true, to_apply=%region_5.6 | all-reduce | flops 1 | bytes 8 | tf_op jit(solution)/shard_map/psum | solution.py:37
  290.2 10.8 %psum.23 = f32[]{:T(128)} all-reduce(f32[]{:T(128)} %psum.22), channel_id=1, replica_groups=mesh['days_0'=4,'days_1'=8,'days_2'=4,'cols'=2] {'days_2'}, use_global_device_ids=true, to_apply=%region_6.7 | all-reduce | flops 1 | bytes 8 | tf_op jit(solution)/shard_map/psum | solution.py:37
  301.6 4.7 %broadcast_divide_fusion = f32[32,32768]{1,0:T(8,128)} fusion(f32[]{:T(128)S(6)} %sqrt.3, f32[32,32768]{1,0:T(8,128)} %copy-done, f32[32768]{0:T(1024)S(1)} %bitcast.17, pred[32]{0:T(512)(128)(4,1)S(1)} %broadcast_compare_fusion), kind=kLoop, calls=%fused_computation.10 | loop fusion | flops 3145728 | bytes 8519716 | tf_op jit(solution)/shard_map/div | solution.py:89
  306.3 0.6 dynamic-slice_divide_fusion
  (13 shorter events, 1.4 us)
Async XLA Ops:
  7.2 162.7 %all-gather.3.cloned.1.call-start = ((), (), s32[]{:S(2)}) async-start(), calls=%async_computation.1 | async-start | bytes 16974336 | tf_op jit(solution)/shard_map/all_gather | solution.py:18
  8.5 8.3 %copy-start.2 = (s32[32]{0:T(128)S(1)}, s32[32]{0:T(128)}, u32[]{:S(2)}) copy-start(s32[32]{0:T(128)} %param.6) | copy-start | bytes 388
  12.9 2.0 copy-start
  204.5 14.8 %copy-start.1 = (f32[32,32768]{1,0:T(8,128)S(1)}, f32[32,32768]{1,0:T(8,128)}, u32[]{:S(2)}) copy-start(f32[32,32768]{1,0:T(8,128)} %copy-done) | copy-start | bytes 12582916
Sparse Core Ops, SparseCore 0:
  16.8 152.9 all-gather.2
where the time goes:
time: 316 us; the launch traced here: 314 us
  waiting for transfers between devices  152 us (48%)
  matrix products  52 us (16%)
  local copies, waits for them, and re-layouts  43.1 us (14%)
  blocking collectives  39.9 us (13%)
  between operations  14.8 us (5%)
  other arithmetic  11.2 us (4%)
    all_gather x1, waiting for transfers between devices, side_by_side(): out = lax.all_gather(both, axis, axis=dim, tiled=True)  152 us
    psum x3, blocking collectives, one_axis_at_a_time(): array = lax.psum(array, axis)  36.1 us
    all_gather x1, local copies, waits for them, and re-layouts, side_by_side(): out = lax.all_gather(both, axis, axis=dim, tiled=True)  34.6 us
    dot_general x8, matrix products, add_block(): jnp.dot(rows, onehot, preferred_element_type=jnp.float32, precision=lax.P...  32.7 us
    dot_general x1, matrix products, body(): jnp.dot(weights[None, :], tails, preferred_element_type=jnp.float32, prec...  14.8 us
  transfers between devices with their start and end apart: 1, of which 1 were waited for; matrix products, arithmetic and copies ran while one was open for 0% of the time, Pallas kernels for 0%

commit v1 on v0

v1 whole, which is shorter than its diff:
```python
import functools

import jax
import jax.numpy as jnp
from jax import lax
from jax.experimental import pallas as pl
from jax.experimental.pallas import tpu as pltpu
from jax.sharding import Mesh
from jax.sharding import PartitionSpec as P

PARENTS = 512
NX, NZH, NZL, NY = 4, 4, 2, 4
GROUP = NX * NZL * NY
CHUNK = 1024
RUN = NZL * NY
F32 = jnp.float32
BF16 = jnp.bfloat16
MESH = pl.DeviceIdType.MESH


def ring(a, n):
    return min(a, n - a)


OFFSETS = sorted(
    [(dx, dz, dy) for dx in range(NX) for dz in range(NZL) for dy in range(NY)][1:],
    key=lambda o: -(ring(o[0], NX) + o[1] + ring(o[2], NY)),
)


def year_tile(years):
    rows = years.shape[1]
    t = lax.broadcasted_iota(jnp.int32, (rows, rows), 0)
    u = lax.broadcasted_iota(jnp.int32, (rows, rows), 1)
    column = jnp.sum(jnp.where(t == u, years.astype(F32), 0.0), axis=1, keepdims=True)
    return jnp.broadcast_to(column, (rows, 128))


def same(a, b):
    return jnp.where(a == b, 1.0, 0.0).astype(F32)


def exchange_kernel(
    entries,
    cube_hbm,
    year_hbm,
    parent_hbm,
    carry_out,
    rollup_out,
    inv_out,
    cube,
    year,
    parent,
    tails,
    ysend,
    yrs1,
    recv1,
    pre1,
    tot,
    ytot,
    recv2,
    yrs2,
    pre2,
    back,
    carry,
    acc,
    part,
    rpart,
    raw,
    rmsg,
    rr,
    rpre,
    rrun,
    rr3,
    rcin,
    qmsg,
    rq,
    load_sem,
    send_sem,
    recv_sem,
):
    days, width = cube.shape
    x, z, y, c = (lax.axis_index(a) for a in ("x", "z", "y", "c"))
    zh, zl = lax.div(z, NZL), lax.rem(z, NZL)
    xs = [lax.rem(x + d, NX) for d in range(NX)]
    zls = [lax.rem(zl + d, NZL) for d in range(NZL)]
    ys = [lax.rem(y + d, NY) for d in range(NY)]
    zhs = [lax.rem(zh + d, NZH) for d in range(NZH)]
    mine = (x * NZL + zl) * NY + y
    peers = [
        (
            {"x": xs[dx], "z": zh * NZL + zls[dz], "y": ys[dy], "c": c},
            (xs[dx] * NZL + zls[dz]) * NY + ys[dy],
        )
        for dx, dz, dy in OFFSETS
    ]
    far = [{"x": x, "z": zhs[d] * NZL + zl, "y": y, "c": c} for d in (2, 1, 3)]
    partner = {"x": x, "z": z, "y": y, "c": 1 - c}

    pieces = 8
    span = width // pieces
    small = [
        pltpu.make_async_copy(year_hbm, year, load_sem.at[pieces]),
        pltpu.make_async_copy(parent_hbm, parent, load_sem.at[pieces + 1]),
    ]
    loads = [
        pltpu.make_async_copy(
            cube_hbm.at[:, pl.ds(k * span, span)], cube.at[:, pl.ds(k * span, span)], load_sem.at[k]
        )
        for k in range(pieces)
    ]
    small[0].start()
    for load in loads:
        load.start()
    small[1].start()

    barrier = pltpu.get_barrier_semaphore()
    for device in [p[0] for p in peers] + far + [partner]:
        pl.semaphore_signal(barrier, inc=1, device_id=device, device_id_type=MESH)

    small[0].wait()
    ytile = year_tile(year[...])
    first, last = ytile[0:1], ytile[days - 1 : days]
    ysend[0:1, :] = first
    ysend[1:2, :] = last
    in_last = ytile == last
    in_first = same(ytile, first)

    for k in range(pieces):
        loads[k].wait()

        def tail_chunk(h, _):
            for s in range(8):
                begin = pl.multiple_of(h * CHUNK + s * 128, 128)
                rows = cube[:, pl.ds(begin, 128)]
                tails[h, s : s + 1, :] = jnp.sum(
                    jnp.where(in_last, rows, 0.0), axis=0, keepdims=True
                )
            return 0

        per = span // CHUNK
        lax.fori_loop(k * per, (k + 1) * per, tail_chunk, 0)

    pl.semaphore_wait(barrier, len(peers) + len(far) + 1)

    def send(src, dst, slot, device):
        copy = pltpu.make_async_remote_copy(
            src_ref=src,
            dst_ref=dst,
            send_sem=send_sem.at[slot],
            recv_sem=recv_sem.at[slot],
            device_id=device,
            device_id_type=MESH,
        )
        copy.start()

    def settle(ref, slot):
        copy = pltpu.make_async_remote_copy(
            src_ref=ref,
            dst_ref=ref,
            send_sem=send_sem.at[slot],
            recv_sem=recv_sem.at[slot],
            device_id=partner,
            device_id_type=MESH,
        )
        return copy

    others = len(peers)
    for device, index in peers:
        send(tails.at[index], recv1.at[mine], 0, device)
    for device, index in peers:
        send(ysend, yrs1.at[mine], 1, device)
    recv1[mine] = tails[mine]
    yrs1[mine] = ysend[...]

    small[1].wait()
    acc[...] = jnp.zeros_like(acc)
    half = PARENTS // 2

    def add_block(j, _):
        begin = pl.multiple_of(j * CHUNK, CHUNK)
        rows = cube[:, pl.ds(begin, CHUNK)]
        owner = parent[:, pl.ds(begin, CHUNK)]
        upper = owner >= half
        place = jnp.where(upper, owner - half, owner)
        low = jnp.where(upper, 0.0, rows)
        both = jnp.concatenate([low, rows - low], axis=0)
        head = both.astype(BF16)
        rest = (both - head.astype(F32)).astype(BF16)
        lhs = jnp.concatenate([head, rest], axis=0)
        targets = lax.broadcasted_iota(jnp.int32, (half, CHUNK), 0)
        onehot = jnp.where(targets == place, 1.0, 0.0).astype(BF16)
        acc[...] += lax.dot_general(
            lhs, onehot, (((1,), (1,)), ((), ())), preferred_element_type=F32
        )
        return 0

    lax.fori_loop(0, width // CHUNK, add_block, 0)
    for h in range(2):
        part[h] = (
            acc[h * days : (h + 1) * days, :] + acc[(h + 2) * days : (h + 3) * days, :]
        )
    send(part.at[1 - c], rpart, 2, partner)

    settle(recv1.at[pl.ds(0, others)], 0).wait_recv()
    settle(yrs1.at[pl.ds(0, others)], 1).wait_recv()
    for g in range(NX):
        run_first = yrs1[g * RUN, 0:1, :]
        total, total_year = None, None
        for k in range(RUN):
            d = g * RUN + k
            d_first, d_last = yrs1[d, 0:1, :], yrs1[d, 1:2, :]
            tile = recv1[d]
            if k == 0:
                pre1[d] = jnp.zeros_like(tile)
                total = tile
            else:
                pre1[d] = total * same(total_year, d_first)
                total = tile + total * same(total_year, d_last)
            total_year = d_last
        tot[g] = total
        ytot[g, 0:1, :] = run_first
        ytot[g, 1:2, :] = total_year
    for device in far:
        send(tot, recv2.at[zh], 3, device)
        send(ytot, yrs2.at[zh], 4, device)
    recv2[zh] = tot[...]
    yrs2[zh] = ytot[...]

    settle(rpart, 2).wait_recv()
    raw[...] = part[c] + rpart[...]
    order = lax.broadcasted_iota(jnp.int32, (days, 128), 0)

    def add_day(u, sums):
        row = raw[pl.ds(u, 1), :]
        year_u = jnp.sum(jnp.where(order == u, ytile, 0.0), axis=0, keepdims=True)
        keep = jnp.where(jnp.logical_and(ytile == year_u, order >= u), 1.0, 0.0)
        return sums[0] + keep * row[:, :128], sums[1] + keep * row[:, 128:]

    zero = jnp.zeros((days, 128), F32)
    loc = lax.fori_loop(0, days, add_day, (zero, zero))
    for i in range(2):
        rmsg[i : i + 1, :] = loc[i][days - 1 : days]
        rmsg[2 + i : 3 + i, :] = jnp.sum(loc[i] * in_first, axis=0, keepdims=True)
    rmsg[4:5, :] = first
    rmsg[5:6, :] = last
    rmsg[6:7, :] = jnp.sum(in_first, axis=0, keepdims=True)
    rmsg[7:8, :] = jnp.sum(loc[0] * loc[0] + loc[1] * loc[1], axis=0, keepdims=True)
    spot = pl.ds(pl.multiple_of(mine * 8, 8), 8)
    for device, index in peers:
        send(rmsg, rr.at[spot], 5, device)
    rr[spot, :] = rmsg[...]

    settle(recv2.at[pl.ds(0, NZH - 1)], 3).wait_recv()
    settle(yrs2.at[pl.ds(0, NZH - 1)], 4).wait_recv()
    total, total_year = None, None
    for g in range(NX):
        for h in range(NZH):
            r_first, r_last = yrs2[h, g, 0:1, :], yrs2[h, g, 1:2, :]
            tile = recv2[h, g]
            if total is None:
                pre2[g * NZH + h] = jnp.zeros_like(tile)
                total = tile
            else:
                pre2[g * NZH + h] = total * same(total_year, r_first)
                total = tile + total * same(total_year, r_last)
            total_year = r_last
    for g in range(NX):
        run_first = yrs1[g * RUN, 0:1, :]
        into = pre2[g * NZH + zh]
        for k in range(RUN):
            d = g * RUN + k
            back[d] = pre1[d] + into * same(yrs1[d, 0:1, :], run_first)
    for device, index in peers:
        send(back.at[index], carry.at[mine], 6, device)
    carry[mine] = back[mine]

    settle(rr.at[pl.ds(0, others * 8)], 5).wait_recv()

    def quantity(ref, row, n):
        return ref[pl.ds(row, n, stride=8), :]

    shape = (NX, RUN, 128)
    t3 = [quantity(rr, i, GROUP).reshape(shape) for i in range(2)]
    s3 = [quantity(rr, 2 + i, GROUP).reshape(shape) for i in range(2)]
    f3, l3, n3, q3 = (quantity(rr, i, GROUP).reshape(shape) for i in range(4, 8))
    rank = lax.broadcasted_iota(jnp.int32, shape, 1)
    pre = [jnp.zeros(shape, F32) for _ in range(2)]
    for k in range(RUN - 1):
        keep = jnp.where(jnp.logical_and(l3[:, k : k + 1] == f3, rank > k), 1.0, 0.0)
        pre = [pre[i] + keep * t3[i][:, k : k + 1] for i in range(2)]
    starts = same(f3, f3[:, 0:1])
    ends = same(l3, l3[:, RUN - 1 : RUN])
    energy = q3
    for i in range(2):
        energy += pre[i] * (2.0 * s3[i] + n3 * pre[i])
        rpre[:, i * 128 : (i + 1) * 128] = pre[i].reshape(GROUP, 128)
    rows = [jnp.sum(ends * t3[i], axis=1) for i in range(2)]
    rows += [jnp.sum(starts * (s3[i] + n3 * pre[i]), axis=1) for i in range(2)]
    rows += [f3[:, 0], l3[:, RUN - 1]]
    rows += [jnp.sum(starts * n3, axis=1), jnp.sum(energy, axis=1)]
    for g in range(NX):
        for i in range(8):
            rrun[g * 8 + i : g * 8 + i + 1, :] = rows[i][g : g + 1]
    spot3 = pl.ds(pl.multiple_of(zh * NX * 8, 8), NX * 8)
    for device in far:
        send(rrun, rr3.at[spot3], 7, device)
    rr3[spot3, :] = rrun[...]

    settle(rr3.at[pl.ds(0, (NZH - 1) * NX * 8)], 7).wait_recv()
    runs = NX * NZH
    t2 = [quantity(rr3, i, runs) for i in range(2)]
    u2 = [quantity(rr3, 2 + i, runs) for i in range(2)]
    f2, l2, n2, q2 = (quantity(rr3, i, runs) for i in range(4, 8))
    position = lax.broadcasted_iota(jnp.int32, (runs, 128), 0)
    turn = (position % NX) * NZH + position // NX
    cin = [jnp.zeros((runs, 128), F32) for _ in range(2)]
    for i in range(runs):
        when = (i % NX) * NZH + i // NX
        keep = jnp.where(jnp.logical_and(l2[i : i + 1] == f2, turn > when), 1.0, 0.0)
        cin = [cin[j] + keep * t2[j][i : i + 1] for j in range(2)]
    energy = q2
    for i in range(2):
        energy += cin[i] * (2.0 * u2[i] + n2 * cin[i])
        rcin[:, i * 128 : (i + 1) * 128] = cin[i]
    qmsg[...] = jnp.broadcast_to(jnp.sum(energy, axis=0, keepdims=True), (8, 128))
    send(qmsg, rq, 8, partner)

    own_run = rcin[pl.ds(zh * NX + x, 1), :]
    own_pre = rpre[pl.ds(mine, 1), :]
    opens = same(first, yrs1[x * RUN, 0:1, :])
    opens = jnp.concatenate([opens, opens], axis=1)
    own = own_pre + opens * own_run
    region = [loc[i] + in_first * own[:, i * 128 : (i + 1) * 128] for i in range(2)]

    settle(rq, 8).wait_recv()
    squares = jnp.sum(qmsg[...] + rq[...], axis=1, keepdims=True)
    inv = jnp.broadcast_to(lax.rsqrt(squares / entries + 1e-06), (8, 128))
    inv_out[...] = inv
    for i in range(2):
        rollup_out[:, i * 128 : (i + 1) * 128] = region[i] * inv[0:1]

    settle(carry.at[pl.ds(0, others)], 6).wait_recv()
    carry_out[...] = carry[...].reshape(GROUP * 8, 128)

    settle(recv1.at[pl.ds(0, others)], 0).wait_send()
    settle(yrs1.at[pl.ds(0, others)], 1).wait_send()
    settle(rpart, 2).wait_send()
    settle(recv2.at[pl.ds(0, NZH - 1)], 3).wait_send()
    settle(yrs2.at[pl.ds(0, NZH - 1)], 4).wait_send()
    settle(rr.at[pl.ds(0, others * 8)], 5).wait_send()
    settle(carry.at[pl.ds(0, others)], 6).wait_send()
    settle(rr3.at[pl.ds(0, (NZH - 1) * NX * 8)], 7).wait_send()
    settle(rq, 8).wait_send()


def exchange(cube, year, parent, entries):
    days, width = cube.shape
    half = PARENTS // 2
    anywhere = pl.BlockSpec(memory_space=pl.ANY)
    vmem = pl.BlockSpec(memory_space=pltpu.VMEM)
    V = lambda *shape: pltpu.VMEM(shape, F32)
    return pl.pallas_call(
        functools.partial(exchange_kernel, entries),
        out_shape=(
            jax.ShapeDtypeStruct((GROUP * 8, 128), F32),
            jax.ShapeDtypeStruct((days, half), F32),
            jax.ShapeDtypeStruct((8, 128), F32),
        ),
        in_specs=[anywhere] * 3,
        out_specs=(vmem,) * 3,
        scratch_shapes=[
            V(days, width),
            pltpu.VMEM((1, days), jnp.int32),
            pltpu.VMEM((1, width), jnp.int32),
            V(GROUP, 8, 128),
            V(2, 128),
            V(GROUP, 2, 128),
            V(GROUP, 8, 128),
            V(GROUP, 8, 128),
            V(NX, 8, 128),
            V(NX, 2, 128),
            V(NZH, NX, 8, 128),
            V(NZH, NX, 2, 128),
            V(NX * NZH, 8, 128),
            V(GROUP, 8, 128),
            V(GROUP, 8, 128),
            V(4 * days, half),
            V(2, days, half),
            V(days, half),
            V(days, half),
            V(8, 128),
            V(GROUP * 8, 128),
            V(GROUP, half),
            V(NX * 8, 128),
            V(NZH * NX * 8, 128),
            V(NX * NZH, half),
            V(8, 128),
            V(8, 128),
            pltpu.SemaphoreType.DMA((10,)),
            pltpu.SemaphoreType.DMA((9,)),
            pltpu.SemaphoreType.DMA((9,)),
        ],
        compiler_params=pltpu.CompilerParams(
            collective_id=0, has_side_effects=True, vmem_limit_bytes=24 * 1024 * 1024
        ),
        name="exchange",
    )(cube, year, parent)


BLOCK = 2048


def finish_kernel(cube, year, carry, small, inv, running, rollup):
    days = cube.shape[0]
    ytile = year_tile(year[...])
    in_first = same(ytile, ytile[0:1])
    order = lax.broadcasted_iota(jnp.int32, (days, 128), 0)
    steps = [s for s in (1, 2, 4, 8, 16) if s < days]
    keeps = [
        jnp.where(jnp.logical_and(order >= s, pltpu.roll(ytile, s, 0) == ytile), 1.0, 0.0)
        for s in steps
    ]
    scale = inv[0:1, :]

    def column(k, _):
        at = pl.ds(pl.multiple_of(k * 128, 128), 128)
        rows = cube[:, at]
        for s, keep in zip(steps, keeps):
            rows = rows + keep * pltpu.roll(rows, s, 0)
        running[:, at] = (rows + in_first * carry[pl.ds(k, 1), :]) * scale
        return 0

    lax.fori_loop(0, BLOCK // 128, column, 0, unroll=2)
    rollup[...] = small[...]


def finish(cube, year, carry, small, inv):
    days, width = cube.shape
    whole = lambda a: pl.BlockSpec(a.shape, lambda k: (0, 0))
    return pl.pallas_call(
        finish_kernel,
        grid=(width // BLOCK,),
        out_shape=(
            jax.ShapeDtypeStruct(cube.shape, F32),
            jax.ShapeDtypeStruct(small.shape, F32),
        ),
        in_specs=[
            pl.BlockSpec((days, BLOCK), lambda k: (0, k)),
            whole(year),
            pl.BlockSpec((BLOCK // 128, 128), lambda k: (k, 0)),
            whole(small),
            whole(inv),
        ],
        out_specs=(pl.BlockSpec((days, BLOCK), lambda k: (0, k)), whole(small)),
        compiler_params=pltpu.CompilerParams(
            dimension_semantics=("arbitrary",), vmem_limit_bytes=16 * 1024 * 1024
        ),
        name="finish",
    )(cube, year, carry, small, inv)


def body(cube, year_id, parent):
    days = cube.shape[0]
    entries = days * NX * NZH * NZL * NY * PARENTS
    year = year_id.reshape(1, -1)
    carry, small, inv = exchange(cube, year, parent.reshape(1, -1), entries)
    return finish(cube, year, carry, small, inv)


def solution(mesh):
    finer = Mesh(mesh.devices.reshape(NX, NZH * NZL, NY, 2), ("x", "z", "y", "c"))
    days = ("x", "z", "y")
    return jax.shard_map(
        body,
        mesh=finer,
        in_specs=(P(days, "c"), P(days), P("c")),
        out_specs=(P(days, "c"), P(days, "c")),
        check_vma=False,
    )
```

time: 316 us -> 48 us (0.15)
  the two profiles are of different devices: /device:TPU:2 before, /device:TPU:1 now
where the time goes in v1:
time: 48 us; the launch traced here: 47.8 us
  Pallas kernels  43.5 us (91%)
  local copies, waits for them, and re-layouts  3.74 us (8%)
  between operations  0.65 us (1%)
    pallas_call x1, Pallas kernels, exchange(): pl.pallas_call(functools.partial(exchange_kernel, entries), out_shape=(ja...  34.9 us
    pallas_call x1, Pallas kernels, finish(): pl.pallas_call(finish_kernel, grid=(width // BLOCK,), out_shape=(jax.Shap...  8.55 us
    unnamed x6, local copies, waits for them, and re-layouts  3.74 us

profile of v1, /device:TPU:1, one launch (start us, length us, event | category | flops | bytes accessed | tf_op | source)
XLA Modules:
  0.0 47.8 jit_solution(7270520929472121129)
XLA Ops:
  0.6 0.0 copy-start
  0.6 2.2 %copy-done = f32[32,32768]{1,0:T(8,128)S(1)} copy-done((f32[32,32768]{1,0:T(8,128)S(1)}, f32[32,32768]{1,0:T(8,128)}, u32[]{:S(2)}) %copy-start) | copy-done | bytes 4194328
  2.8 0.0 copy-start.1
  2.8 0.9 %copy-done.1 = s32[32768]{0:T(1024)S(1)} copy-done((s32[32768]{0:T(1024)S(1)}, s32[32768]{0:T(1024)}, u32[]{:S(2)}) %copy-start.1) | copy-done | bytes 131096
  3.7 0.0 copy-start.2
  3.7 0.7 %copy-done.2 = s32[32]{0:T(128)S(1)} copy-done((s32[32]{0:T(128)S(1)}, s32[32]{0:T(128)}, u32[]{:S(2)}) %copy-start.2) | copy-done | bytes 152
  4.4 34.9 %exchange.1 = (f32[256,128]{1,0:T(8,128)S(1)}, f32[32,256]{1,0:T(8,128)S(1)}, f32[8,128]{1,0:T(8,128)S(1)}) custom-call(f32[32,32768]{1,0:T(8,128)S(1)} %copy-done, s32[1,32]{1,0:T(1,128)S(1)} %bitcast.3, s32[1,32768]{1,0:T(1,128)S(1)} %bitcast.2), custom_call_target="tpu_custom_call" | custom-call | tf_op jit(solution)/shard_map/exchange/pallas_call | solution.py:363
  39.3 8.5 %finish.1 = (f32[32,32768]{1,0:T(8,128)}, f32[32,256]{1,0:T(8,128)}) custom-call(f32[32,32768]{1,0:T(8,128)S(1)} %copy-done, s32[1,32]{1,0:T(1,128)S(1)} %bitcast.4, f32[256,128]{1,0:T(8,128)S(1)} %get-tuple-element.5.carry, f32[32,256]{1,0:T(8,128)S(1)} %get-tuple-element.6.small, f32[8,128]{1,0:T(8,128)S(1)} %get-tuple-element.7.inv), custom_call_target="tpu_custom_call" | custom-call | tf_op jit(solution)/shard_map/finish/pallas_call | solution.py:441
Async XLA Ops:
  0.6 2.2 %copy-start = (f32[32,32768]{1,0:T(8,128)S(1)}, f32[32,32768]{1,0:T(8,128)}, u32[]{:S(2)}) copy-start(f32[32,32768]{1,0:T(8,128)} %cube.1) | copy-start | bytes 12582916
  2.8 0.9 %copy-start.1 = (s32[32768]{0:T(1024)S(1)}, s32[32768]{0:T(1024)}, u32[]{:S(2)}) copy-start(s32[32768]{0:T(1024)} %param.5) | copy-start | bytes 393220
  3.7 0.7 %copy-start.2 = (s32[32]{0:T(128)S(1)}, s32[32]{0:T(128)}, u32[]{:S(2)}) copy-start(s32[32]{0:T(128)} %param.4) | copy-start | bytes 388

commit v2 on v1

--- a/solution.py
+++ b/solution.py
@@ -45,10 +45,10 @@
     cube_hbm,
     year_hbm,
     parent_hbm,
+    cube,
     carry_out,
     rollup_out,
-    inv_out,
-    cube,
+    factors_out,
     year,
     parent,
     tails,
@@ -66,7 +66,6 @@
     acc,
     part,
     rpart,
-    raw,
     rmsg,
     rr,
     rpre,
@@ -123,8 +122,14 @@
     first, last = ytile[0:1], ytile[days - 1 : days]
     ysend[0:1, :] = first
     ysend[1:2, :] = last
-    in_last = ytile == last
     in_first = same(ytile, first)
+    ybyte = ytile.reshape(days // 8, 8, 128)
+    order = lax.broadcasted_iota(jnp.int32, (days // 8, 8, 128), 1)
+    keeps = [
+        jnp.where(jnp.logical_and(order >= s, pltpu.roll(ybyte, s, 1) == ybyte), 1.0, 0.0)
+        for s in (1, 2, 4)
+    ]
+    joins = [same(ybyte[i], ybyte[i - 1, 7:8]) for i in range(1, days // 8)]
 
     for k in range(pieces):
         loads[k].wait()
@@ -132,10 +137,15 @@
         def tail_chunk(h, _):
             for s in range(8):
                 begin = pl.multiple_of(h * CHUNK + s * 128, 128)
-                rows = cube[:, pl.ds(begin, 128)]
-                tails[h, s : s + 1, :] = jnp.sum(
-                    jnp.where(in_last, rows, 0.0), axis=0, keepdims=True
-                )
+                rows = cube[:, pl.ds(begin, 128)].reshape(days // 8, 8, 128)
+                for shift, keep in zip((1, 2, 4), keeps):
+                    rows = rows + keep * pltpu.roll(rows, shift, 1)
+                groups = [rows[0]]
+                for i, join in enumerate(joins):
+                    groups.append(rows[i + 1] + join * groups[-1][7:8])
+                for i, group in enumerate(groups):
+                    cube[i * 8 : i * 8 + 8, pl.ds(begin, 128)] = group
+                tails[h, s : s + 1, :] = groups[-1][7:8]
             return 0
 
         per = span // CHUNK
@@ -155,7 +165,7 @@
         copy.start()
 
     def settle(ref, slot):
-        copy = pltpu.make_async_remote_copy(
+        return pltpu.make_async_remote_copy(
             src_ref=ref,
             dst_ref=ref,
             send_sem=send_sem.at[slot],
@@ -163,7 +173,6 @@
             device_id=partner,
             device_id_type=MESH,
         )
-        return copy
 
     others = len(peers)
     for device, index in peers:
@@ -228,17 +237,7 @@
     yrs2[zh] = ytot[...]
 
     settle(rpart, 2).wait_recv()
-    raw[...] = part[c] + rpart[...]
-    order = lax.broadcasted_iota(jnp.int32, (days, 128), 0)
-
-    def add_day(u, sums):
-        row = raw[pl.ds(u, 1), :]
-        year_u = jnp.sum(jnp.where(order == u, ytile, 0.0), axis=0, keepdims=True)
-        keep = jnp.where(jnp.logical_and(ytile == year_u, order >= u), 1.0, 0.0)
-        return sums[0] + keep * row[:, :128], sums[1] + keep * row[:, 128:]
-
-    zero = jnp.zeros((days, 128), F32)
-    loc = lax.fori_loop(0, days, add_day, (zero, zero))
+    loc = [part[c, :, i * 128 : i * 128 + 128] + rpart[:, i * 128 : i * 128 + 128] for i in range(2)]
     for i in range(2):
         rmsg[i : i + 1, :] = loc[i][days - 1 : days]
         rmsg[2 + i : 3 + i, :] = jnp.sum(loc[i] * in_first, axis=0, keepdims=True)
@@ -336,7 +335,8 @@
     settle(rq, 8).wait_recv()
     squares = jnp.sum(qmsg[...] + rq[...], axis=1, keepdims=True)
     inv = jnp.broadcast_to(lax.rsqrt(squares / entries + 1e-06), (8, 128))
-    inv_out[...] = inv
+    factors_out[0:8, :] = inv
+    factors_out[8 : 8 + days, :] = in_first * inv[0:1]
     for i in range(2):
         rollup_out[:, i * 128 : (i + 1) * 128] = region[i] * inv[0:1]
 
@@ -357,20 +357,20 @@
 def exchange(cube, year, parent, entries):
     days, width = cube.shape
     half = PARENTS // 2
-    anywhere = pl.BlockSpec(memory_space=pl.ANY)
+    hbm = pl.BlockSpec(memory_space=pltpu.HBM)
     vmem = pl.BlockSpec(memory_space=pltpu.VMEM)
     V = lambda *shape: pltpu.VMEM(shape, F32)
     return pl.pallas_call(
         functools.partial(exchange_kernel, entries),
         out_shape=(
+            jax.ShapeDtypeStruct((days, width), F32),
             jax.ShapeDtypeStruct((GROUP * 8, 128), F32),
             jax.ShapeDtypeStruct((days, half), F32),
-            jax.ShapeDtypeStruct((8, 128), F32),
+            jax.ShapeDtypeStruct((8 + days, 128), F32),
         ),
-        in_specs=[anywhere] * 3,
-        out_specs=(vmem,) * 3,
+        in_specs=[hbm] * 3,
+        out_specs=(vmem,) * 4,
         scratch_shapes=[
-            V(days, width),
             pltpu.VMEM((1, days), jnp.int32),
             pltpu.VMEM((1, width), jnp.int32),
             V(GROUP, 8, 128),
@@ -388,7 +388,6 @@
             V(4 * days, half),
             V(2, days, half),
             V(days, half),
-            V(days, half),
             V(8, 128),
             V(GROUP * 8, 128),
             V(GROUP, half),
@@ -405,67 +404,61 @@
             collective_id=0, has_side_effects=True, vmem_limit_bytes=24 * 1024 * 1024
         ),
         name="exchange",
-    )(cube, year, parent)
-
-
-BLOCK = 2048
-
-
-def finish_kernel(cube, year, carry, small, inv, running, rollup):
-    days = cube.shape[0]
-    ytile = year_tile(year[...])
-    in_first = same(ytile, ytile[0:1])
-    order = lax.broadcasted_iota(jnp.int32, (days, 128), 0)
-    steps = [s for s in (1, 2, 4, 8, 16) if s < days]
-    keeps = [
-        jnp.where(jnp.logical_and(order >= s, pltpu.roll(ytile, s, 0) == ytile), 1.0, 0.0)
-        for s in steps
-    ]
-    scale = inv[0:1, :]
-
-    def column(k, _):
-        at = pl.ds(pl.multiple_of(k * 128, 128), 128)
-        rows = cube[:, at]
-        for s, keep in zip(steps, keeps):
-            rows = rows + keep * pltpu.roll(rows, s, 0)
-        running[:, at] = (rows + in_first * carry[pl.ds(k, 1), :]) * scale
-        return 0
-
-    lax.fori_loop(0, BLOCK // 128, column, 0, unroll=2)
-    rollup[...] = small[...]
-
-
-def finish(cube, year, carry, small, inv):
-    days, width = cube.shape
-    whole = lambda a: pl.BlockSpec(a.shape, lambda k: (0, 0))
+    )(*(pltpu.with_memory_space_constraint(a, pltpu.HBM) for a in (cube, year, parent)))
+
+
+PIECES = 8
+
+
+def finish_kernel(local, carry, small, factors, running, rollup, stage, sems):
+    days, width = local.shape
+    span = width // PIECES
+    last = pltpu.make_async_copy(small, rollup, sems.at[PIECES])
+    last.start()
+    scale, opening = factors[0:1, :], factors[8 : 8 + days, :]
+    copies = []
+    for piece in range(PIECES):
+
+        def column(k, _):
+            at = pl.ds(pl.multiple_of(k * 128, 128), 128)
+            stage[:, at] = local[:, at] * scale + opening * carry[pl.ds(k, 1), :]
+            return 0
+
+        per = span // 128
+        lax.fori_loop(piece * per, (piece + 1) * per, column, 0, unroll=4)
+        at = pl.ds(piece * span, span)
+        copies.append(pltpu.make_async_copy(stage.at[:, at], running.at[:, at], sems.at[piece]))
+        copies[-1].start()
+    for copy in copies + [last]:
+        copy.wait()
+
+
+def finish(local, carry, small, factors):
+    vmem = pl.BlockSpec(memory_space=pltpu.VMEM)
+    hbm = pl.BlockSpec(memory_space=pltpu.HBM)
     return pl.pallas_call(
         finish_kernel,
-        grid=(width // BLOCK,),
         out_shape=(
-            jax.ShapeDtypeStruct(cube.shape, F32),
+            jax.ShapeDtypeStruct(local.shape, F32),
             jax.ShapeDtypeStruct(small.shape, F32),
         ),
-        in_specs=[
-            pl.BlockSpec((days, BLOCK), lambda k: (0, k)),
-            whole(year),
-            pl.BlockSpec((BLOCK // 128, 128), lambda k: (k, 0)),
-            whole(small),
-            whole(inv),
+        in_specs=[vmem] * 4,
+        out_specs=(hbm, hbm),
+        scratch_shapes=[
+            pltpu.VMEM(local.shape, F32),
+            pltpu.SemaphoreType.DMA((PIECES + 1,)),
         ],
-        out_specs=(pl.BlockSpec((days, BLOCK), lambda k: (0, k)), whole(small)),
-        compiler_params=pltpu.CompilerParams(
-            dimension_semantics=("arbitrary",), vmem_limit_bytes=16 * 1024 * 1024
-        ),
+        compiler_params=pltpu.CompilerParams(vmem_limit_bytes=16 * 1024 * 1024),
         name="finish",
-    )(cube, year, carry, small, inv)
+    )(local, carry, small, factors)
 
 
 def body(cube, year_id, parent):
     days = cube.shape[0]
     entries = days * NX * NZH * NZL * NY * PARENTS
     year = year_id.reshape(1, -1)
-    carry, small, inv = exchange(cube, year, parent.reshape(1, -1), entries)
-    return finish(cube, year, carry, small, inv)
+    local, carry, small, factors = exchange(cube, year, parent.reshape(1, -1), entries)
+    return finish(local, carry, small, factors)
 
 
 def solution(mesh):

time: 48 us -> 41.8 us (0.87)
  local copies, waits for them, and re-layouts: 3.74 us -> 0 us
  Pallas kernels: 43.5 us -> 41 us
    pallas_call x1, Pallas kernels: 8.55 us -> 2.21 us  [finish(): pl.pallas_call(finish_kernel, out_shape=(jax.ShapeDtypeStruct(local.shape...]
    pallas_call x1, Pallas kernels: 34.9 us -> 38.8 us  [exchange(): pl.pallas_call(functools.partial(exchange_kernel, entries), out_shape=(ja...]
    unnamed x6 -> x0, local copies, waits for them, and re-layouts: 3.74 us -> none
where the time goes in v2:
time: 41.8 us; the launch traced here: 41.7 us
  Pallas kernels  41 us (98%)
  between operations  0.64 us (2%)
    pallas_call x1, Pallas kernels, exchange(): pl.pallas_call(functools.partial(exchange_kernel, entries), out_shape=(ja...  38.8 us
    pallas_call x1, Pallas kernels, finish(): pl.pallas_call(finish_kernel, out_shape=(jax.ShapeDtypeStruct(local.shape...  2.21 us

profile of v2, /device:TPU:1, one launch (start us, length us, event | category | flops | bytes accessed | tf_op | source)
XLA Modules:
  0.0 41.7 jit_solution(9063577223760998527)
XLA Ops:
  0.6 38.8 %exchange.1 = (f32[32,32768]{1,0:T(8,128)S(1)}, f32[256,128]{1,0:T(8,128)S(1)}, f32[32,256]{1,0:T(8,128)S(1)}, f32[40,128]{1,0:T(8,128)S(1)}) custom-call(f32[32,32768]{1,0:T(8,128)} %cube_hbm.1, s32[1,32]{1,0:T(1,128)} %bitcast.3, s32[1,32768]{1,0:T(1,128)} %bitcast.2), custom_call_target="tpu_custom_call" | custom-call | tf_op jit(solution)/shard_map/exchange/pallas_call | solution.py:363
  39.5 2.2 %finish.1 = (f32[32,32768]{1,0:T(8,128)}, f32[32,256]{1,0:T(8,128)}) custom-call(f32[32,32768]{1,0:T(8,128)S(1)} %get-tuple-element.6.local, f32[256,128]{1,0:T(8,128)S(1)} %get-tuple-element.7.carry, f32[32,256]{1,0:T(8,128)S(1)} %get-tuple-element.8.small, f32[40,128]{1,0:T(8,128)S(1)} %get-tuple-element.9.factors), custom_call_target="tpu_custom_call" | custom-call | tf_op jit(solution)/shard_map/finish/pallas_call | solution.py:439

commit v3 on v2

--- a/solution.py
+++ b/solution.py
@@ -12,6 +12,7 @@
 NX, NZH, NZL, NY = 4, 4, 2, 4
 GROUP = NX * NZL * NY
 CHUNK = 1024
+PER = 16
 RUN = NZL * NY
 F32 = jnp.float32
 BF16 = jnp.bfloat16
@@ -38,6 +39,17 @@
 
 def same(a, b):
     return jnp.where(a == b, 1.0, 0.0).astype(F32)
+
+
+def prefix_rows(rows, keeps, joins):
+    days = rows.shape[0]
+    rows = rows.reshape(days // 8, 8, 128)
+    for shift, keep in zip((1, 2, 4), keeps):
+        rows = rows + keep * pltpu.roll(rows, shift, 1)
+    groups = [rows[0]]
+    for i, join in enumerate(joins):
+        groups.append(rows[i + 1] + join * groups[-1][7:8])
+    return groups
 
 
 def exchange_kernel(
@@ -131,25 +143,19 @@
     ]
     joins = [same(ybyte[i], ybyte[i - 1, 7:8]) for i in range(1, days // 8)]
 
+    in_last = ytile == last
     for k in range(pieces):
         loads[k].wait()
 
         def tail_chunk(h, _):
             for s in range(8):
                 begin = pl.multiple_of(h * CHUNK + s * 128, 128)
-                rows = cube[:, pl.ds(begin, 128)].reshape(days // 8, 8, 128)
-                for shift, keep in zip((1, 2, 4), keeps):
-                    rows = rows + keep * pltpu.roll(rows, shift, 1)
-                groups = [rows[0]]
-                for i, join in enumerate(joins):
-                    groups.append(rows[i + 1] + join * groups[-1][7:8])
-                for i, group in enumerate(groups):
-                    cube[i * 8 : i * 8 + 8, pl.ds(begin, 128)] = group
-                tails[h, s : s + 1, :] = groups[-1][7:8]
+                rows = jnp.where(in_last, cube[:, pl.ds(begin, 128)], 0.0)
+                tails[h, s : s + 1, :] = jnp.sum(rows, axis=0, keepdims=True)
             return 0
 
         per = span // CHUNK
-        lax.fori_loop(k * per, (k + 1) * per, tail_chunk, 0)
+        lax.fori_loop(k * per, (k + 1) * per, tail_chunk, 0, unroll=2)
 
     pl.semaphore_wait(barrier, len(peers) + len(far) + 1)
 
@@ -186,25 +192,26 @@
     acc[...] = jnp.zeros_like(acc)
     half = PARENTS // 2
 
+    WIDE = 4096
+    targets = lax.broadcasted_iota(jnp.int32, (half, WIDE), 0).astype(BF16)
     def add_block(j, _):
-        begin = pl.multiple_of(j * CHUNK, CHUNK)
-        rows = cube[:, pl.ds(begin, CHUNK)]
-        owner = parent[:, pl.ds(begin, CHUNK)]
+        begin = pl.multiple_of(j * WIDE, WIDE)
+        rows = cube[:, pl.ds(begin, WIDE)]
+        owner = parent[:, pl.ds(begin, WIDE)]
         upper = owner >= half
-        place = jnp.where(upper, owner - half, owner)
+        place = jnp.where(upper, owner - half, owner).astype(F32).astype(BF16)
         low = jnp.where(upper, 0.0, rows)
         both = jnp.concatenate([low, rows - low], axis=0)
         head = both.astype(BF16)
         rest = (both - head.astype(F32)).astype(BF16)
         lhs = jnp.concatenate([head, rest], axis=0)
-        targets = lax.broadcasted_iota(jnp.int32, (half, CHUNK), 0)
-        onehot = jnp.where(targets == place, 1.0, 0.0).astype(BF16)
+        onehot = jnp.where(targets == place, jnp.ones((), BF16), jnp.zeros((), BF16)).astype(jnp.float8_e4m3fn)
         acc[...] += lax.dot_general(
             lhs, onehot, (((1,), (1,)), ((), ())), preferred_element_type=F32
         )
         return 0
 
-    lax.fori_loop(0, width // CHUNK, add_block, 0)
+    lax.fori_loop(0, width // WIDE, add_block, 0)
     for h in range(2):
         part[h] = (
             acc[h * days : (h + 1) * days, :] + acc[(h + 2) * days : (h + 3) * days, :]
@@ -237,7 +244,10 @@
     yrs2[zh] = ytot[...]
 
     settle(rpart, 2).wait_recv()
-    loc = [part[c, :, i * 128 : i * 128 + 128] + rpart[:, i * 128 : i * 128 + 128] for i in range(2)]
+    loc = []
+    for i in range(2):
+        at = slice(i * 128, i * 128 + 128)
+        loc.append(jnp.concatenate(prefix_rows(part[c, :, at] + rpart[:, at], keeps, joins), axis=0))
     for i in range(2):
         rmsg[i : i + 1, :] = loc[i][days - 1 : days]
         rmsg[2 + i : 3 + i, :] = jnp.sum(loc[i] * in_first, axis=0, keepdims=True)
@@ -249,6 +259,15 @@
     for device, index in peers:
         send(rmsg, rr.at[spot], 5, device)
     rr[spot, :] = rmsg[...]
+
+    def column(k, _):
+        for s in range(PER):
+            at = pl.ds(pl.multiple_of((k * PER + s) * 128, 128), 128)
+            for i, group in enumerate(prefix_rows(cube[:, at], keeps, joins)):
+                cube[i * 8 : i * 8 + 8, at] = group
+        return 0
+
+    lax.fori_loop(0, width // 128 // PER, column, 0)
 
     settle(recv2.at[pl.ds(0, NZH - 1)], 3).wait_recv()
     settle(yrs2.at[pl.ds(0, NZH - 1)], 4).wait_recv()

time: 41.8 us -> 32.9 us (0.79)
  Pallas kernels: 41 us -> 32.2 us
    pallas_call x1, Pallas kernels: 38.8 us -> 30 us  [exchange(): pl.pallas_call(functools.partial(exchange_kernel, entries), out_shape=(ja...]
where the time goes in v3:
time: 32.9 us; the launch traced here: 32.8 us
  Pallas kernels  32.2 us (98%)
  between operations  0.64 us (2%)
    pallas_call x1, Pallas kernels, exchange(): pl.pallas_call(functools.partial(exchange_kernel, entries), out_shape=(ja...  30 us
    pallas_call x1, Pallas kernels, finish(): pl.pallas_call(finish_kernel, out_shape=(jax.ShapeDtypeStruct(local.shape...  2.21 us

profile of v3, /device:TPU:1, one launch (start us, length us, event | category | flops | bytes accessed | tf_op | source)
XLA Modules:
  0.0 32.8 jit_solution(10603415472607660477)
XLA Ops:
  0.6 30.0 %exchange.1 = (f32[32,32768]{1,0:T(8,128)S(1)}, f32[256,128]{1,0:T(8,128)S(1)}, f32[32,256]{1,0:T(8,128)S(1)}, f32[40,128]{1,0:T(8,128)S(1)}) custom-call(f32[32,32768]{1,0:T(8,128)} %cube_hbm.1, s32[1,32]{1,0:T(1,128)} %bitcast.3, s32[1,32768]{1,0:T(1,128)} %bitcast.2), custom_call_target="tpu_custom_call" | custom-call | tf_op jit(solution)/shard_map/exchange/pallas_call | solution.py:382
  30.6 2.2 %finish.1 = (f32[32,32768]{1,0:T(8,128)}, f32[32,256]{1,0:T(8,128)}) custom-call(f32[32,32768]{1,0:T(8,128)S(1)} %get-tuple-element.6.local, f32[256,128]{1,0:T(8,128)S(1)} %get-tuple-element.7.carry, f32[32,256]{1,0:T(8,128)S(1)} %get-tuple-element.8.small, f32[40,128]{1,0:T(8,128)S(1)} %get-tuple-element.9.factors), custom_call_target="tpu_custom_call" | custom-call | tf_op jit(solution)/shard_map/finish/pallas_call | solution.py:458
